TPU v7x, 32 devices: a whole 2x2x4 slice. The times are simulated.
32 devices in a mesh: gx: 4 (over x, core), gy: 2 (over y), gz: 4 (over z).
Axes of the slice: x: 2, y: 2, z: 4, core: 2. Of those that a mesh axis runs over, the one named last changes fastest.
Arguments:
- velocity: float32 [3, 128, 192, 1024], P(None, 'gx', 'gy', 'gz'), may hold values from -6 to 6
Outputs:
- magnitude: float32 [128, 192, 1024], P('gx', ('gy', 'gz'))
- level_one: float32 [64, 96, 512], P('gx', 'gy')
- level_two: float32 [32, 48, 256], P('gx', 'gy')
- level_three: float32 [16, 24, 128], P('gx', 'gy')
- level_four: float32 [8, 12, 64], P('gx', 'gy')
- level_five: float32 [4, 6, 32], P('gx', 'gy')
All inputs are finite; a program needn't handle non-finite values.
Results may differ from a plain program's by a relative error of at most 0.000075.
Values sent between devices are 32-bit elements; how exact they have to be, the bound alone decides.
A program may use at most 256 MiB of HBM per device.

v0:
```python
import jax
import jax.numpy as jnp
from jax import lax
from jax.sharding import PartitionSpec as P


def extended(value, sides, width):
    for axis, dim in sides:
        peers, length = (lax.axis_size(axis), value.shape[dim])
        up = [(i, (i + 1) % peers) for i in range(peers)]
        down = [(j, i) for i, j in up]
        last = lax.slice_in_dim(value, length - width, length, axis=dim)
        leading = lax.slice_in_dim(value, 0, width, axis=dim)
        before = lax.ppermute(last, axis, up)
        after = lax.ppermute(leading, axis, down)
        value = jnp.concatenate([before, value, after], axis=dim)
    return value


def depth_diff(field, before, after):
    ahead = jnp.roll(field, -1, 2)
    behind = jnp.roll(field, 1, 2)
    depth_index = lax.broadcasted_iota(jnp.int32, field.shape, 2)
    ahead = jnp.where(depth_index == field.shape[2] - 1, after[:, :, None], ahead)
    behind = jnp.where(depth_index == 0, before[:, :, None], behind)
    return (ahead - behind) * 0.5


def vorticity(padded, before, after):
    inner = padded[:, 1:-1, 1:-1, :]

    def first_diff(comp):
        return (padded[comp, 2:, 1:-1, :] - padded[comp, :-2, 1:-1, :]) * 0.5

    def second_diff(comp):
        return (padded[comp, 1:-1, 2:, :] - padded[comp, 1:-1, :-2, :]) * 0.5

    def third_diff(comp):
        return depth_diff(inner[comp], before[comp], after[comp])

    curl_first = second_diff(2) - third_diff(1)
    curl_second = third_diff(0) - first_diff(2)
    curl_third = first_diff(1) - second_diff(0)
    return jnp.sqrt(
        1.0 + curl_first * curl_first + curl_second * curl_second + curl_third * curl_third
    )


def pooled(field):
    rows, cols, depth = field.shape
    summed = field.reshape(rows // 2, 2, cols, depth).sum(axis=1)
    summed = summed.reshape(rows // 2, cols // 2, 2, depth).sum(axis=2)
    pairing = (
        lax.broadcasted_iota(jnp.int32, (depth, depth // 2), 0) // 2
        == lax.broadcasted_iota(jnp.int32, (depth, depth // 2), 1)
    ).astype(jnp.float32)
    merged = jnp.dot(
        summed.reshape(-1, depth),
        pairing,
        precision=lax.Precision.HIGHEST,
        preferred_element_type=jnp.float32,
    )
    return merged.reshape(rows // 2, cols // 2, depth // 2) * 0.125


def end_planes(velocity):
    return jnp.concatenate([velocity[..., :1], velocity[..., -1:]], axis=3)


def on_device(velocity):
    padded = extended(velocity, (("gx", 1), ("gy", 2)), 1)
    planes = extended(end_planes(velocity), (("gz", 3),), 1)
    block_mag = vorticity(padded, planes[..., 0], planes[..., 3])
    pencil = lax.all_to_all(block_mag, "gz", split_axis=1, concat_axis=2, tiled=True)
    level_one = lax.all_gather(pooled(pencil), "gz", axis=1, tiled=True)
    level_two = pooled(level_one)
    level_three = pooled(level_two)
    level_four = pooled(level_three)
    level_five = pooled(level_four)
    return (pencil, level_one, level_two, level_three, level_four, level_five)


def solution(mesh):
    in_specs = (P(None, "gx", "gy", "gz"),)
    out_specs = (
        P("gx", ("gy", "gz"), None),
        P("gx", "gy", None),
        P("gx", "gy", None),
        P("gx", "gy", None),
        P("gx", "gy", None),
        P("gx", "gy", None),
    )
    return jax.shard_map(
        on_device, mesh=mesh, in_specs=in_specs, out_specs=out_specs, check_vma=False
    )
```

profile of v0, /device:TPU:0, one launch (start us, length us, event | category | flops | bytes accessed | tf_op | source)
XLA Modules:
  0.0 252.0 jit_solution(13280708438288536689)
XLA Ops:
  7.2 1.1 fusion.61
  8.3 1.0 copy.103
  9.3 2.4 collective-permute-start.1
  11.7 1.0 copy.102
  12.8 8.7 %fusion.60 = (f32[3,32,96,1]{3,2,1,0:T(8,128)}, f32[3,32,96,1]{3,2,1,0:T(8,128)}) fusion(f32[3,32,96,256]{3,2,1,0:T(8,128)} %param.1), kind=kLoop, calls=%fused_computation.114 | loop fusion | bytes 147456 | tf_op jit(solution)/shard_map/slice | solution.py:67
  21.5 3.1 %copy.129 = f32[3,32,96,1]{2,1,3,0:T(8,128)S(1)} copy(f32[3,32,96,1]{3,2,1,0:T(8,128)} %get-tuple-element.51) | data formatting | bytes 73728
  24.6 1.6 collective-permute-start.5
  26.2 3.1 %copy.128 = f32[3,32,96,1]{2,1,3,0:T(8,128)S(1)} copy(f32[3,32,96,1]{3,2,1,0:T(8,128)} %get-tuple-element.50) | data formatting | bytes 73728
  29.3 2.5 collective-permute-start.4
  31.8 16.0 %constant_dynamic-update-slice_fusion = (f32[3,33,96,256]{3,1,2,0:T(8,128)}, f32[3,32,96,256]{3,1,2,0:T(8,128)}) fusion(f32[3,32,96,256]{3,2,1,0:T(8,128)} %param.1), kind=kLoop, calls=%fused_computation.93 | loop fusion | bytes 28311552
  47.7 3.6 %slice_bitcast_fusion = (f32[32,96,256]{2,0,1:T(8,128)S(1)}, f32[32,96,256]{2,0,1:T(8,128)S(1)}) fusion(f32[3,32,96,256]{3,1,2,0:T(8,128)} %get-tuple-element.55), kind=kLoop, calls=%fused_computation.22 | loop fusion | bytes 12582912 | tf_op jit(solution)/shard_map/squeeze | solution.py:39
  51.3 3.7 %fusion.62 = (f32[32,96,1]{2,0,1:T(8,128)}, f32[32,96,1]{2,0,1:T(8,128)}, f32[32,96,1]{2,0,1:T(8,128)}, f32[32,96,1]{2,0,1:T(8,128)}) fusion(f32[32,96,256]{2,0,1:T(8,128)S(1)} %get-tuple-element.52, f32[32,96,256]{2,0,1:T(8,128)S(1)} %get-tuple-element.53), kind=kLoop, calls=%fused_computation.116 | loop fusion | bytes 98304 | tf_op jit(solution)/shard_map/jit(_roll_static)/slice | solution.py:22
  55.0 6.5 %fusion.63 = (f32[32,96,255]{2,0,1:T(8,128)}, f32[32,96,255]{2,0,1:T(8,128)}, f32[32,96,255]{2,0,1:T(8,128)}, f32[32,96,255]{2,0,1:T(8,128)}) fusion(f32[32,96,256]{2,0,1:T(8,128)S(1)} %get-tuple-element.52, f32[32,96,256]{2,0,1:T(8,128)S(1)} %get-tuple-element.53), kind=kLoop, calls=%fused_computation.117 | loop fusion | bytes 25067520 | tf_op jit(solution)/shard_map/jit(_roll_static)/slice | solution.py:22
  61.6 0.5 iota_compare_fusion.6
  62.1 0.7 slice_bitcast_fusion.4
  62.8 1.8 pad_maximum_fusion.9
  64.7 1.5 collective-permute-start.2
  66.2 0.5 collective-permute-start.3
  66.7 1.3 slice_bitcast_fusion.5
  68.0 0.1 copy.109
  68.1 0.1 copy.112
  68.2 1.4 copy.106
  69.6 1.4 copy.110
  71.1 7.8 %dynamic-update-slice.1 = f32[3,33,96,256]{3,1,2,0:T(8,128)} dynamic-update-slice(f32[3,33,96,256]{3,1,2,0:T(8,128)} %get-tuple-element.54, f32[3,1,96,256]{3,1,2,0:T(1,128)S(1)} %collective-permute-done.1, s32[]{} %constant.86, s32[]{} %constant.87, s32[]{} %constant.86, s32[]{} %constant.86) | dynamic-update-slice | bytes 589828 | tf_op jit(solution)/shard_map/concatenate | solution.py:16
  78.9 21.6 %fusion.6 = f32[32,96,256]{2,0,1:T(8,128)} fusion(f32[3,34,1,256]{3,1,2,0:T(8,128)} %collective-permute-done.3, f32[3,1,96,256]{3,1,2,0:T(1,128)S(1)} %collective-permute-done.1, f32[3,32,96,256]{3,1,2,0:T(8,128)} %get-tuple-element.55, f32[3,1,96,256]{3,1,2,0:T(1,128)} %collective-permute-done, f32[3,34,1,256]{3,1,2,0:T(8,128)} %collective-permute-done.2, ...), kind=kLoop, calls=%fused_computation.7 | loop fusion | flops 33816576 | bytes 32305664 | tf_op jit(solution)/shard_map/sqrt | solution.py:44
  100.5 3.7 %all-to-all-start = ((f32[32,96,256]{2,0,1:T(8,128)}), f32[32,96,256]{2,0,1:T(8,128)S(1)}, u32[]{:S(2)}, u32[]{:S(2)}) async-start(f32[32,96,256]{2,0,1:T(8,128)} %fusion.6), calls=%async_computation | async-start | bytes 6291456 | tf_op jit(solution)/shard_map/all_to_all | solution.py:74
  104.2 0.0 all-gather.2.cloned.1.call-start
  104.3 70.6 %all-to-all-done = f32[32,96,256]{2,0,1:T(8,128)S(1)} async-done(((f32[32,96,256]{2,0,1:T(8,128)}), f32[32,96,256]{2,0,1:T(8,128)S(1)}, u32[]{:S(2)}, u32[]{:S(2)}) %all-to-all-start) | async-done | bytes 3145760 | tf_op jit(solution)/shard_map/all_to_all | solution.py:74
  175.0 1.7 copy-done.1
  176.6 3.9 %copy.145 = f32[32,4,24,256]{3,1,2,0:T(4,128)S(1)} copy(f32[32,4,24,256]{3,0,2,1:T(8,128)} %bitcast.78) | data formatting | bytes 6291456 | tf_op jit(solution)/shard_map/all_to_all | solution.py:74
  180.5 3.3 %reshape.90 = f32[16,2,24,1024]{3,2,1,0:T(8,128)} reshape(f32[32,24,4,256]{3,2,1,0:T(4,128)S(1)} %bitcast.76) | data formatting | bytes 6291456 | tf_op jit(solution)/shard_map/reshape | solution.py:51
  183.8 3.5 %reduce_sum.90 = f32[16,24,1024]{2,1,0:T(8,128)} reduce(f32[16,2,24,1024]{3,2,1,0:T(8,128)} %reshape.90, f32[]{:T(128)} %constant.81.clone.1), dimensions={1}, to_apply=%region_0.1 | reduce | flops 393216 | bytes 4718596 | tf_op jit(solution)/shard_map/reduce_sum | solution.py:51
  187.3 3.5 %copy.126 = f32[16,24,1024]{2,0,1:T(8,128)} copy(f32[16,24,1024]{2,1,0:T(8,128)} %reduce_sum.90) | data formatting | bytes 3145728 | tf_op jit(solution)/shard_map/reshape | solution.py:52
  190.8 2.5 reduce_sum.91
  193.2 3.0 %fusion.26 = f32[16,12,512]{2,0,1:T(8,128)} fusion(f32[16,12,1024]{2,0,1:T(8,128)} %reduce_sum.91, s32[1024]{0:T(1024)S(1)} %get-tuple-element.82, s32[1024]{0:T(1024)S(1)} %get-tuple-element.83, pred[1024]{0:T(1024)(128)(4,1)S(1)} %fusion.56), kind=kOutput, calls=%fused_computation.42 | convolution fusion | flops 1209106432 | bytes 1188864 | tf_op jit(solution)/shard_map/dot_general | solution.py:57
  196.4 3.0 %all_to_all.16 = f32[32,24,1024]{2,1,0:T(8,128)} reshape(f32[32,24,4,256]{3,2,1,0:T(4,128)S(1)} %bitcast.77) | data formatting | bytes 6291456 | tf_op jit(solution)/shard_map/all_to_all | solution.py:74
  199.4 33.1 %all-gather.2.cloned.1.call-done = f32[16,48,512]{2,0,1:T(8,128)} async-done(((f32[16,12,512]{2,0,1:T(8,128)}), f32[16,48,512]{2,0,1:T(8,128)}) %all-gather.2.cloned.1.call-update) | async-done | bytes 1572880 | tf_op jit(solution)/shard_map/all_gather | solution.py:75
  232.6 2.2 reshape.92
  234.8 3.0 %reduce_sum.92 = f32[8,48,512]{2,0,1:T(8,128)} reduce(f32[8,2,48,512]{3,1,0,2:T(2,128)S(1)} %reshape.92, f32[]{:T(128)} %constant.81.clone.1), dimensions={1}, to_apply=%region_2.3 | reduce | flops 196608 | bytes 2359300 | tf_op jit(solution)/shard_map/reduce_sum | solution.py:51
  237.8 1.2 reduce_sum.93
  239.0 1.4 bitcast_reduce_fusion
  240.5 0.3 bitcast_reduce_fusion.1
  240.9 0.1 fusion.66
  241.1 0.2 fusion.29
  241.3 0.6 copy.125
  241.9 0.6 copy.124
  242.5 0.6 copy.123
  243.1 2.1 copy.122
  (29 shorter events, 0.2 us)
Async XLA Ops:
  9.3 53.5 %collective-permute-start.1 = (f32[3,1,96,256]{3,1,2,0:T(1,128)}, f32[3,1,96,256]{3,1,2,0:T(1,128)S(1)}, u32[]{:S(2)}, u32[]{:S(2)}) collective-permute-start(f32[3,1,96,256]{3,1,2,0:T(1,128)} %copy.103), channel_id=1, source_target_pairs={{8,0},{16,8},{24,16},{0,24},{9,1},{17,9},{25,17},{1,25},{10,2},{18... | collective-permute-start | bytes 884744 | tf_op jit(solution)/shard_map/ppermute | solution.py:15
  12.8 50.1 %collective-permute-start = (f32[3,1,96,256]{3,1,2,0:T(1,128)}, f32[3,1,96,256]{3,1,2,0:T(1,128)}, u32[]{:S(2)}, u32[]{:S(2)}) collective-permute-start(f32[3,1,96,256]{3,1,2,0:T(1,128)} %copy.102), channel_id=1, source_target_pairs={{0,8},{8,16},{16,24},{24,0},{1,9},{9,17},{17,25},{25,1},{2,10},{10... | collective-permute-start | bytes 884744 | tf_op jit(solution)/shard_map/ppermute | solution.py:14
  24.6 37.5 %collective-permute-start.5 = (f32[3,32,96,1]{2,1,3,0:T(8,128)S(1)}, f32[3,32,96,1]{2,1,3,0:T(8,128)}, u32[]{:S(2)}, u32[]{:S(2)}) collective-permute-start(f32[3,32,96,1]{2,1,3,0:T(8,128)S(1)} %copy.129), channel_id=1, source_target_pairs={{0,1},{1,2},{2,3},{3,0},{4,5},{5,6},{6,7},{7,4},{8,9},{9,10},{10,1... | collective-permute-start | bytes 110600 | tf_op jit(solution)/shard_map/ppermute | solution.py:14
  29.3 37.4 %collective-permute-start.4 = (f32[3,32,96,1]{2,1,3,0:T(8,128)S(1)}, f32[3,32,96,1]{2,1,3,0:T(8,128)}, u32[]{:S(2)}, u32[]{:S(2)}) collective-permute-start(f32[3,32,96,1]{2,1,3,0:T(8,128)S(1)} %copy.128), channel_id=1, source_target_pairs={{1,0},{2,1},{3,2},{0,3},{5,4},{6,5},{7,6},{4,7},{9,8},{10,9},{11,1... | collective-permute-start | bytes 110600 | tf_op jit(solution)/shard_map/ppermute | solution.py:15
  62.8 16.1 %copy-start = (f32[32,96,255]{2,0,1:T(8,128)S(1)}, f32[32,96,255]{2,0,1:T(8,128)}, u32[]{:S(2)}) copy-start(f32[32,96,255]{2,0,1:T(8,128)} %get-tuple-element.60) | copy-start | bytes 9400324
  64.7 14.2 %collective-permute-start.2 = (f32[3,34,1,256]{3,1,2,0:T(8,128)}, f32[3,34,1,256]{3,1,2,0:T(8,128)}, u32[]{:S(2)}, u32[]{:S(2)}) collective-permute-start(f32[3,34,1,256]{3,1,2,0:T(8,128)} %get-tuple-element.48), channel_id=1, source_target_pairs={{4,0},{0,4},{5,1},{1,5},{6,2},{2,6},{7,3},{3,7},{12,8},{8,12},{13,... | collective-permute-start | bytes 313352 | tf_op jit(solution)/shard_map/ppermute | solution.py:15
  66.2 12.7 %collective-permute-start.3 = (f32[3,34,1,256]{3,1,2,0:T(8,128)}, f32[3,34,1,256]{3,1,2,0:T(8,128)}, u32[]{:S(2)}, u32[]{:S(2)}) collective-permute-start(f32[3,34,1,256]{3,1,2,0:T(8,128)} %get-tuple-element.49), channel_id=1, source_target_pairs={{0,4},{4,0},{1,5},{5,1},{2,6},{6,2},{3,7},{7,3},{8,12},{12,8},{9,1... | collective-permute-start | bytes 313352 | tf_op jit(solution)/shard_map/ppermute | solution.py:14
  100.5 74.4 %all-to-all-start = ((f32[32,96,256]{2,0,1:T(8,128)}), f32[32,96,256]{2,0,1:T(8,128)S(1)}, u32[]{:S(2)}, u32[]{:S(2)}) async-start(f32[32,96,256]{2,0,1:T(8,128)} %fusion.6), calls=%async_computation | async-start | bytes 6291456 | tf_op jit(solution)/shard_map/all_to_all | solution.py:74
  104.2 128.3 %all-gather.2.cloned.1.call-start = ((), (), s32[]{:S(2)}) async-start(), calls=%async_computation.1 | async-start | bytes 1966080 | tf_op jit(solution)/shard_map/all_gather | solution.py:75
  175.0 1.7 copy-start.1
  234.8 8.3 %copy-start.2 = (f32[16,48,512]{2,0,1:T(8,128)S(1)}, f32[16,48,512]{2,0,1:T(8,128)}, u32[]{:S(2)}) copy-start(f32[16,48,512]{2,0,1:T(8,128)} %all-gather.2.cloned.1.call-done) | copy-start | bytes 4718596
Sparse Core Ops, SparseCore 0:
  196.4 36.0 all-gather.1
where the time goes:
time: 253 us; the launch traced here: 252 us
  waiting for transfers between devices  104 us (41%)
  local copies, waits for them, and re-layouts  82.3 us (33%)
  other arithmetic  34.2 us (14%)
  between operations  14.2 us (6%)
  starting transfers between devices  12.3 us (5%)
  matrix products  5.12 us (2%)
    all_to_all x1, waiting for transfers between devices, on_device(): lax.all_to_all(block_mag, 'gz', split_axis=1, concat_axis=2, tiled=True)  70.6 us
    all_gather x1, waiting for transfers between devices, on_device(): level_one = lax.all_gather(pooled(pencil), 'gz', axis=1, tiled=True)  33.1 us
    unnamed x13, local copies, waits for them, and re-layouts  27.7 us
    sqrt x1, other arithmetic, vorticity(): jnp.sqrt(1.0 + curl_first * curl_first + curl_second * curl_second + curl...  21.6 us
    slice x2, local copies, waits for them, and re-layouts, depth_diff(): behind = jnp.roll(field, 1, 2)  10.2 us
    slice x1, local copies, waits for them, and re-layouts, end_planes(): return jnp.concatenate([velocity[..., :1], velocity[..., -1:]], axis=3)  8.69 us
    concatenate x1, local copies, waits for them, and re-layouts, extended(): value = jnp.concatenate([before, value, after], axis=dim)  7.82 us
    all_to_all x2, local copies, waits for them, and re-layouts, on_device(): lax.all_to_all(block_mag, 'gz', split_axis=1, concat_axis=2, tiled=True)  6.95 us
  transfers between devices with their start and end apart: 8, of which 2 were waited for; matrix products, arithmetic and copies ran while one was open for 24% of the time, Pallas kernels for 0%

commit v1 on v0

--- a/solution.py
+++ b/solution.py
@@ -71,7 +71,16 @@
     padded = extended(velocity, (("gx", 1), ("gy", 2)), 1)
     planes = extended(end_planes(velocity), (("gz", 3),), 1)
     block_mag = vorticity(padded, planes[..., 0], planes[..., 3])
-    pencil = lax.all_to_all(block_mag, "gz", split_axis=1, concat_axis=2, tiled=True)
+
+    def remake_the_node(q_in, k_dim, dimension_no=2):
+        raw_out = lax.psum(1, axis_name="gz")
+        a_next = jnp.split(q_in, raw_out, k_dim)
+        z2 = jnp.stack(a_next, axis=0)
+        heard = lax.all_to_all(z2, axis_name="gz", split_axis=0, concat_axis=0)
+        upper = jnp.concatenate(heard, dimension_no)
+        return upper
+
+    pencil = remake_the_node(block_mag, 1)
     level_one = lax.all_gather(pooled(pencil), "gz", axis=1, tiled=True)
     level_two = pooled(level_one)
     level_three = pooled(level_two)

time: 253 us -> 245 us (0.968)
  local copies, waits for them, and re-layouts: 82.3 us -> 75.3 us
  other arithmetic: 34.2 us -> 29 us
  waiting for transfers between devices: 104 us -> 107 us
    slice x2, local copies, waits for them, and re-layouts: 10.2 us -> 17.2 us  [depth_diff(): behind = jnp.roll(field, 1, 2)]
    concatenate x1, local copies, waits for them, and re-layouts: 7.82 us -> 0.87 us  [extended(): value = jnp.concatenate([before, value, after], axis=dim)]
    all_to_all x2 -> x0, local copies, waits for them, and re-layouts: 6.95 us -> none  [on_device(): lax.all_to_all(block_mag, 'gz', split_axis=1, concat_axis=2, tiled=True)]
    reshape x0 -> x2, local copies, waits for them, and re-layouts: none -> 5.83 us  [remake_the_node(): upper = jnp.concatenate(heard, dimension_no)]
    another operation x0 -> x2, local copies, waits for them, and re-layouts: none -> 5.47 us  [the longest x1 5.23 us: pooled(): summed = field.reshape(rows // 2, 2, cols, depth).sum(axis=1)]
    unnamed x13 -> x20, local copies, waits for them, and re-layouts: 27.7 us -> 22.5 us
    sqrt x1, other arithmetic: 21.6 us -> 16.8 us  [vorticity(): jnp.sqrt(1.0 + curl_first * curl_first + curl_second * curl_second + curl...]
    broadcast_in_dim x3 -> x1, local copies, waits for them, and re-layouts: 4.2 us -> 0.01 us  [depth_diff(): jnp.where(depth_index == field.shape[2] - 1, after[:, :, None], ahead)]
  transfers between devices with their start and end apart: 8 -> 8, of which waited for: 2 -> 4; matrix products, arithmetic and copies ran while one was open for 24% -> 23% of each run, Pallas kernels for 0% -> 0%
where the time goes in v1:
time: 245 us; the launch traced here: 244 us
  waiting for transfers between devices  107 us (44%)
  local copies, waits for them, and re-layouts  75.3 us (31%)
  other arithmetic  29 us (12%)
  between operations  14.2 us (6%)
  starting transfers between devices  13.9 us (6%)
  matrix products  5.1 us (2%)
    all_to_all x1, waiting for transfers between devices, remake_the_node(): heard = lax.all_to_all(z2, axis_name='gz', split_axis=0, concat_axis=0)  69.4 us
    all_gather x1, waiting for transfers between devices, on_device(): level_one = lax.all_gather(pooled(pencil), 'gz', axis=1, tiled=True)  32.9 us
    unnamed x20, local copies, waits for them, and re-layouts  22.5 us
    slice x2, local copies, waits for them, and re-layouts, depth_diff(): behind = jnp.roll(field, 1, 2)  17.2 us
    sqrt x1, other arithmetic, vorticity(): jnp.sqrt(1.0 + curl_first * curl_first + curl_second * curl_second + curl...  16.8 us
    slice x1, local copies, waits for them, and re-layouts, end_planes(): return jnp.concatenate([velocity[..., :1], velocity[..., -1:]], axis=3)  8.74 us
    ppermute x3, starting transfers between devices, extended(): after = lax.ppermute(leading, axis, down)  7.96 us
    reduce_sum x2, other arithmetic, pooled(): summed = field.reshape(rows // 2, 2, cols, depth).sum(axis=1)  6.46 us
  transfers between devices with their start and end apart: 8, of which 4 were waited for; matrix products, arithmetic and copies ran while one was open for 23% of the time, Pallas kernels for 0%

profile of v1, /device:TPU:0, one launch (start us, length us, event | category | flops | bytes accessed | tf_op | source)
XLA Modules:
  0.0 244.4 jit_solution(10105554741993692881)
XLA Ops:
  7.2 1.1 fusion.61
  8.3 0.5 collective-permute-start
  8.8 2.0 collective-permute-start.1
  10.8 8.7 %fusion.60 = (f32[3,32,96,1]{3,2,1,0:T(8,128)}, f32[3,32,96,1]{3,2,1,0:T(8,128)}) fusion(f32[3,32,96,256]{3,2,1,0:T(8,128)} %param.1), kind=kLoop, calls=%fused_computation.117 | loop fusion | bytes 147456 | tf_op jit(solution)/shard_map/slice | solution.py:67
  19.5 3.1 %copy.69 = f32[3,32,96,1]{2,1,3,0:T(8,128)S(1)} copy(f32[3,32,96,1]{3,2,1,0:T(8,128)} %get-tuple-element.44) | data formatting | bytes 73728
  22.6 4.4 %collective-permute-start.4 = (f32[3,32,96,1]{2,1,3,0:T(8,128)S(1)}, f32[3,32,96,1]{2,1,3,0:T(8,128)S(1)}, u32[]{:S(2)}, u32[]{:S(2)}) collective-permute-start(f32[3,32,96,1]{2,1,3,0:T(8,128)S(1)} %copy.69), channel_id=1, source_target_pairs={{1,0},{2,1},{3,2},{0,3},{5,4},{6,5},{7,6},{4,7},{9,8},{10,9},{11,1... | collective-permute-start | bytes 110600 | tf_op jit(solution)/shard_map/ppermute | solution.py:15
  27.0 3.1 %copy.70 = f32[3,32,96,1]{2,1,3,0:T(8,128)S(1)} copy(f32[3,32,96,1]{3,2,1,0:T(8,128)} %get-tuple-element.45) | data formatting | bytes 73728
  30.1 0.0 collective-permute-start.5
  30.2 6.3 %slice_bitcast_fusion = (f32[32,96,256]{2,1,0:T(8,128)}, f32[32,96,256]{2,1,0:T(8,128)}) fusion(f32[3,32,96,256]{3,2,1,0:T(8,128)} %param.1), kind=kLoop, calls=%fused_computation.32 | loop fusion | bytes 12582912 | tf_op jit(solution)/shard_map/squeeze | solution.py:39
  36.5 11.1 %fusion.63 = (f32[32,96,255]{2,1,0:T(8,128)}, f32[32,96,255]{2,1,0:T(8,128)}, f32[32,96,255]{2,1,0:T(8,128)}, f32[32,96,255]{2,1,0:T(8,128)}) fusion(f32[32,96,256]{2,1,0:T(8,128)} %get-tuple-element.46, f32[32,96,256]{2,1,0:T(8,128)} %get-tuple-element.47), kind=kLoop, calls=%fused_computation.120 | loop fusion | bytes 25067520 | tf_op jit(solution)/shard_map/jit(_roll_static)/slice | solution.py:22
  47.6 6.1 %fusion.62 = (f32[32,96,1]{2,1,0:T(8,128)S(1)}, f32[32,96,1]{2,1,0:T(8,128)}, f32[32,96,1]{2,1,0:T(8,128)}, f32[32,96,1]{2,1,0:T(8,128)}) fusion(f32[32,96,256]{2,1,0:T(8,128)} %get-tuple-element.46, f32[32,96,256]{2,1,0:T(8,128)} %get-tuple-element.47), kind=kLoop, calls=%fused_computation.119 | loop fusion | bytes 98304 | tf_op jit(solution)/shard_map/jit(_roll_static)/slice | solution.py:22
  53.7 0.0 collective-permute-done.4
  53.7 0.0 collective-permute-done
  53.7 0.9 constant_dynamic-update-slice_fusion.6
  54.6 11.5 %constant_dynamic-update-slice_fusion.4 = (f32[3,33,96,256]{3,2,1,0:T(8,128)}, f32[3,34,96,256]{3,2,1,0:T(8,128)}, f32[3,33,96,256]{3,2,1,0:T(8,128)}) fusion(f32[3,32,96,256]{3,2,1,0:T(8,128)S(1)} %bitcast.84, f32[3,34,96,256]{3,2,1,0:T(8,128)} %get-tuple-element.68, f32[3,33,96,256]{3,2,1,0:T(8,128)} %get-tuple-element.67), kind=kLoop, calls=%fused_computation.75 | loop fusion | bytes 37748736
  66.1 0.0 collective-permute-done.1
  66.1 0.9 constant_dynamic-update-slice_fusion.3
  67.0 1.6 fusion.59
  68.6 1.6 collective-permute-start.2
  70.1 0.5 collective-permute-start.3
  70.6 0.0 collective-permute-done.5
  70.7 3.6 %collective-permute-done.2 = f32[3,34,1,256]{3,2,1,0:T(1,128)S(1)} collective-permute-done((f32[3,34,1,256]{3,2,1,0:T(1,128)S(1)}, f32[3,34,1,256]{3,2,1,0:T(1,128)S(1)}, u32[]{:S(2)}, u32[]{:S(2)}) %collective-permute-start.2) | collective-permute-done | bytes 104480 | tf_op jit(solution)/shard_map/ppermute | solution.py:15
  74.3 1.1 collective-permute-done.3
  75.4 16.8 %fusion.6 = f32[32,96,256]{2,1,0:T(8,128)S(1)} fusion(f32[3,34,96,256]{3,2,1,0:T(8,128)} %get-tuple-element.66, f32[3,34,1,256]{3,2,1,0:T(1,128)S(1)} %collective-permute-done.3, f32[3,34,1,256]{3,2,1,0:T(1,128)S(1)} %collective-permute-done.2, f32[3,33,96,256]{3,2,1,0:T(8,128)} %get-tuple-element.50, f32[3,33,96,256]{3,2,1,0:T(8,128)} %get-tuple-element.65, ...), kind=kLoop, calls=%fused_computation.7 | loop fusion | flops 25952256 | bytes 38597120 | tf_op jit(solution)/shard_map/sqrt | solution.py:44
  92.2 0.2 slice_bitcast_fusion.5
  92.4 1.9 pad_maximum_fusion.2
  94.3 4.8 %all-to-all-start = ((f32[4,32,24,256]{3,2,1,0:T(8,128)}), f32[4,32,24,256]{3,2,1,0:T(8,128)S(1)}, u32[]{:S(2)}, u32[]{:S(2)}) async-start(f32[4,32,24,256]{3,2,1,0:T(8,128)} %pad_maximum_fusion.2), calls=%async_computation | async-start | bytes 6291456 | tf_op jit(solution)/shard_map/all_to_all | solution.py:79
  99.1 69.4 %all-to-all-done = f32[4,32,24,256]{3,2,1,0:T(8,128)S(1)} async-done(((f32[4,32,24,256]{3,2,1,0:T(8,128)}), f32[4,32,24,256]{3,2,1,0:T(8,128)S(1)}, u32[]{:S(2)}, u32[]{:S(2)}) %all-to-all-start) | async-done | bytes 3145760 | tf_op jit(solution)/shard_map/all_to_all | solution.py:79
  168.5 3.7 %copy.55 = f32[32,24,4,256]{3,2,1,0:T(4,128)} copy(f32[32,24,4,256]{3,1,0,2:T(8,128)S(1)} %bitcast.85) | data formatting | bytes 6291456 | tf_op jit(solution)/shard_map/reshape | solution.py:80
  172.2 5.2 %reshape_reshape.3 = f32[16,2,24,1024]{3,2,1,0:T(8,128)} reshape(f32[32,24,4,256]{3,2,1,0:T(4,128)} %copy.55) | data formatting | bytes 6291456 | tf_op jit(solution)/shard_map/reshape;reshape | solution.py:51
  177.4 3.5 %reduce_sum.90 = f32[16,24,1024]{2,1,0:T(8,128)} reduce(f32[16,2,24,1024]{3,2,1,0:T(8,128)} %reshape_reshape.3, f32[]{:T(128)} %constant.81.clone.1), dimensions={1}, to_apply=%region_0.1 | reduce | flops 393216 | bytes 4718596 | tf_op jit(solution)/shard_map/reduce_sum | solution.py:51
  180.9 3.5 %copy.67 = f32[16,24,1024]{2,0,1:T(8,128)} copy(f32[16,24,1024]{2,1,0:T(8,128)} %reduce_sum.90) | data formatting | bytes 3145728 | tf_op jit(solution)/shard_map/reshape | solution.py:52
  184.4 2.5 %reduce_sum.91 = f32[16,12,1024]{2,0,1:T(8,128)} reduce(f32[16,12,2,1024]{3,0,2,1:T(8,128)} %bitcast.87, f32[]{:T(128)} %constant.81.clone.1), dimensions={2}, to_apply=%region_1.2 | reduce | flops 196608 | bytes 2359300 | tf_op jit(solution)/shard_map/reduce_sum | solution.py:52
  186.8 3.0 %fusion.25 = f32[16,12,512]{2,0,1:T(8,128)} fusion(f32[16,12,1024]{2,0,1:T(8,128)} %reduce_sum.91, s32[1024]{0:T(1024)S(1)} %get-tuple-element.85, s32[1024]{0:T(1024)S(1)} %get-tuple-element.86, pred[1024]{0:T(1024)(128)(4,1)S(1)} %fusion.55), kind=kOutput, calls=%fused_computation.37 | convolution fusion | flops 1209106432 | bytes 1188864 | tf_op jit(solution)/shard_map/dot_general | solution.py:57
  189.9 0.0 all-gather.2.cloned.1.call-update
  190.0 2.1 copy.71
  192.1 32.9 %all-gather.2.cloned.1.call-done = f32[16,48,512]{2,0,1:T(8,128)} async-done(((f32[16,12,512]{2,0,1:T(8,128)}), f32[16,48,512]{2,0,1:T(8,128)}) %all-gather.2.cloned.1.call-update) | async-done | bytes 1572880 | tf_op jit(solution)/shard_map/all_gather | solution.py:84
  225.0 2.2 reshape.95
  227.3 3.0 %reduce_sum.92 = f32[8,48,512]{2,0,1:T(8,128)} reduce(f32[8,2,48,512]{3,1,0,2:T(2,128)S(1)} %reshape.95, f32[]{:T(128)} %constant.81.clone.1), dimensions={1}, to_apply=%region_2.3 | reduce | flops 196608 | bytes 2359300 | tf_op jit(solution)/shard_map/reduce_sum | solution.py:51
  230.2 1.2 reduce_sum.93
  231.5 1.4 bitcast_reduce_fusion
  232.9 0.3 bitcast_reduce_fusion.1
  233.3 0.1 fusion.66
  233.5 0.2 fusion.28
  233.7 0.6 copy.66
  234.3 0.6 copy.65
  234.9 0.6 copy.64
  235.5 2.1 copy.63
  (33 shorter events, 0.2 us)
Async XLA Ops:
  8.3 45.4 %collective-permute-start = (f32[3,1,96,256]{3,2,1,0:T(8,128)S(1)}, f32[3,1,96,256]{3,2,1,0:T(8,128)S(1)}, u32[]{:S(2)}, u32[]{:S(2)}) collective-permute-start(f32[3,1,96,256]{3,2,1,0:T(8,128)S(1)} %get-tuple-element.52), channel_id=1, source_target_pairs={{0,8},{8,16},{16,24},{24,0},{1,9},{9,17},{17,25},{25,1},{2,10},{10... | collective-permute-start | bytes 884744 | tf_op jit(solution)/shard_map/ppermute | solution.py:14
  8.8 57.3 %collective-permute-start.1 = (f32[3,1,96,256]{3,2,1,0:T(8,128)S(1)}, f32[3,1,96,256]{3,2,1,0:T(8,128)S(1)}, u32[]{:S(2)}, u32[]{:S(2)}) collective-permute-start(f32[3,1,96,256]{3,2,1,0:T(8,128)S(1)} %get-tuple-element.51), channel_id=1, source_target_pairs={{8,0},{16,8},{24,16},{0,24},{9,1},{17,9},{25,17},{1,25},{10,2},{18... | collective-permute-start | bytes 884744 | tf_op jit(solution)/shard_map/ppermute | solution.py:15
  22.6 31.0 %collective-permute-start.4 = (f32[3,32,96,1]{2,1,3,0:T(8,128)S(1)}, f32[3,32,96,1]{2,1,3,0:T(8,128)S(1)}, u32[]{:S(2)}, u32[]{:S(2)}) collective-permute-start(f32[3,32,96,1]{2,1,3,0:T(8,128)S(1)} %copy.69), channel_id=1, source_target_pairs={{1,0},{2,1},{3,2},{0,3},{5,4},{6,5},{7,6},{4,7},{9,8},{10,9},{11,1... | collective-permute-start | bytes 110600 | tf_op jit(solution)/shard_map/ppermute | solution.py:15
  30.1 40.5 %collective-permute-start.5 = (f32[3,32,96,1]{2,1,3,0:T(8,128)S(1)}, f32[3,32,96,1]{2,1,3,0:T(8,128)S(1)}, u32[]{:S(2)}, u32[]{:S(2)}) collective-permute-start(f32[3,32,96,1]{2,1,3,0:T(8,128)S(1)} %copy.70), channel_id=1, source_target_pairs={{0,1},{1,2},{2,3},{3,0},{4,5},{5,6},{6,7},{7,4},{8,9},{9,10},{10,1... | collective-permute-start | bytes 110600 | tf_op jit(solution)/shard_map/ppermute | solution.py:14
  36.5 18.1 %slice-start = ((s8[9437184]{0:T(1024)(128)(4,1)}), s8[4194304]{0:T(1024)(128)(4,1)S(1)}, s32[]{:S(2)}) async-start(s8[9437184]{0:T(1024)(128)(4,1)} %bitcast.83), calls=%async_computation.2 | async-start | bytes 8388608
  36.5 18.1 %slice-start.1 = ((s8[9437184]{0:T(1024)(128)(4,1)}), s8[1048576]{0:T(1024)(128)(4,1)S(1)}, s32[]{:S(2)}) async-start(s8[9437184]{0:T(1024)(128)(4,1)} %bitcast.83), calls=%async_computation.3 | async-start | bytes 2097152
  47.6 7.0 %slice-start.2 = ((s8[9437184]{0:T(1024)(128)(4,1)}), s8[4194304]{0:T(1024)(128)(4,1)S(1)}, s32[]{:S(2)}) async-start(s8[9437184]{0:T(1024)(128)(4,1)} %bitcast.83), calls=%async_computation.4 | async-start | bytes 8388608
  54.6 20.8 %copy-start = (f32[32,96,255]{2,1,0:T(8,128)S(1)}, f32[32,96,255]{2,1,0:T(8,128)}, u32[]{:S(2)}) copy-start(f32[32,96,255]{2,1,0:T(8,128)} %get-tuple-element.59) | copy-start | bytes 9400324
  54.6 20.8 %copy-start.1 = (f32[32,96,255]{2,1,0:T(8,128)S(1)}, f32[32,96,255]{2,1,0:T(8,128)}, u32[]{:S(2)}) copy-start(f32[32,96,255]{2,1,0:T(8,128)} %get-tuple-element.60) | copy-start | bytes 9400324
  68.6 5.7 %collective-permute-start.2 = (f32[3,34,1,256]{3,2,1,0:T(1,128)S(1)}, f32[3,34,1,256]{3,2,1,0:T(1,128)S(1)}, u32[]{:S(2)}, u32[]{:S(2)}) collective-permute-start(f32[3,34,1,256]{3,2,1,0:T(1,128)S(1)} %get-tuple-element.42), channel_id=1, source_target_pairs={{4,0},{0,4},{5,1},{1,5},{6,2},{2,6},{7,3},{3,7},{12,8},{8,12},{13,... | collective-permute-start | bytes 313352 | tf_op jit(solution)/shard_map/ppermute | solution.py:15
  70.1 5.3 %collective-permute-start.3 = (f32[3,34,1,256]{3,2,1,0:T(1,128)S(1)}, f32[3,34,1,256]{3,2,1,0:T(1,128)S(1)}, u32[]{:S(2)}, u32[]{:S(2)}) collective-permute-start(f32[3,34,1,256]{3,2,1,0:T(1,128)S(1)} %get-tuple-element.43), channel_id=1, source_target_pairs={{0,4},{4,0},{1,5},{5,1},{2,6},{6,2},{3,7},{7,3},{8,12},{12,8},{9,1... | collective-permute-start | bytes 313352 | tf_op jit(solution)/shard_map/ppermute | solution.py:14
  94.3 74.2 %all-to-all-start = ((f32[4,32,24,256]{3,2,1,0:T(8,128)}), f32[4,32,24,256]{3,2,1,0:T(8,128)S(1)}, u32[]{:S(2)}, u32[]{:S(2)}) async-start(f32[4,32,24,256]{3,2,1,0:T(8,128)} %pad_maximum_fusion.2), calls=%async_computation | async-start | bytes 6291456 | tf_op jit(solution)/shard_map/all_to_all | solution.py:79
  99.1 125.9 %all-gather.2.cloned.1.call-start = ((), (), s32[]{:S(2)}) async-start(), calls=%async_computation.1 | async-start | bytes 1966080 | tf_op jit(solution)/shard_map/all_gather | solution.py:84
  227.2 8.3 %copy-start.2 = (f32[16,48,512]{2,0,1:T(8,128)S(1)}, f32[16,48,512]{2,0,1:T(8,128)}, u32[]{:S(2)}) copy-start(f32[16,48,512]{2,0,1:T(8,128)} %all-gather.2.cloned.1.call-done) | copy-start | bytes 4718596
Sparse Core Ops, SparseCore 0:
  190.0 34.9 all-gather.1
